TPU v7x, 32 devices: a whole 2x2x4 slice. The times are simulated.
32 devices in a mesh: wide: 16 (over z, y, x), narrow: 2 (over core).
Axes of the slice: x: 2, y: 2, z: 4, core: 2. Of those that a mesh axis runs over, the one named last changes fastest.
Arguments:
- tokens: bfloat16 [2048, 2048], P('wide'), may hold values from -6 to 6
- expert_ids: int32 [2048, 6], P('wide'), may hold values from 0 to 15, all different within a row; in each aligned block of 128 rows (0 to 127, 128 to 255, ...) at most 64 rows name the same one
- gate_weights: float32 [2048, 6], P('wide'), may hold values from 0.05 to 0.6
- shared_gate: bfloat16 [2048, 2816], P('wide', 'narrow'), may hold values from -0.125 to 0.125
- shared_up: bfloat16 [2048, 2816], P('wide', 'narrow'), may hold values from -0.125 to 0.125
- shared_down: bfloat16 [2816, 2048], P('narrow', 'wide'), may hold values from -0.109375 to 0.109375
- expert_gate: bfloat16 [16, 2048, 1408], P('wide', None, 'narrow'), may hold values from -0.125 to 0.125
- expert_up: bfloat16 [16, 2048, 1408], P('wide', None, 'narrow'), may hold values from -0.125 to 0.125
- expert_down: bfloat16 [16, 1408, 2048], P('wide', 'narrow'), may hold values from -0.15625 to 0.15625
Outputs:
- moe_out: bfloat16 [2048, 2048], P('wide', 'narrow')
Inputs may be any that keep to these rules, and one draw needn't show every extreme that they name: `expert_ids`: the 6 ids of a row differ. Among the 128 rows of one index of wide, no expert is named by more than 64 rows.
All inputs are finite; a program needn't handle non-finite values.
Results may differ from a plain program's by a relative error of at most 0.0075.
Values may be sent and summed in bfloat16 or wider, within the bound.
A program may use at most 128 MiB of HBM per device.

v0:
```python
import functools

import jax
import jax.numpy as jnp
from jax import lax
from jax.experimental import pallas as pl
from jax.experimental.pallas import tpu as pltpu
from jax.sharding import PartitionSpec as P


def expert_ffn(received, w_gate, w_up, w_down):
    senders, items, width = received.shape
    flat_rows = received.reshape(senders * items, width)
    gate_part = jnp.dot(flat_rows, w_gate, preferred_element_type=jnp.float32)
    up_part = jnp.dot(flat_rows, w_up, preferred_element_type=jnp.float32)
    hidden = (jax.nn.silu(gate_part) * up_part).astype(jnp.bfloat16)
    partial_value = jnp.dot(hidden, w_down, preferred_element_type=jnp.float32).astype(jnp.bfloat16)
    return partial_value.reshape(senders, items, w_down.shape[1])


def dispatch_body(
    tokens,
    expert_ids,
    gate_weights,
    shared_gate,
    shared_up,
    shared_down,
    expert_gate,
    expert_up,
    expert_down,
):
    tok_count, width = tokens.shape
    top_count = expert_ids.shape[1]
    experts = lax.axis_size("wide") * expert_gate.shape[0]
    capacity = min(tok_count, 4 * tok_count * top_count // (3 * experts))
    narrow_count = lax.axis_size("narrow")
    w_gate = expert_gate[0]
    w_up = expert_up[0]
    w_down = expert_down[0]
    pairs = tok_count * top_count
    flat_ids = expert_ids.reshape(pairs)
    onehot = (flat_ids[:, None] == jnp.arange(experts, dtype=jnp.int32)[None, :]).astype(jnp.int32)
    before = jnp.cumsum(onehot, axis=0) - onehot
    slot_pos = jnp.sum(before * onehot, axis=1)
    target_slot = flat_ids * capacity + slot_pos
    source = (
        jnp.full((experts * capacity,), -1, jnp.int32)
        .at[target_slot]
        .set(jnp.arange(pairs, dtype=jnp.int32))
    )
    filled = source >= 0
    token_of = jnp.where(filled, source // top_count, 0)
    outgoing = jnp.where(filled[:, None], tokens[token_of], jnp.zeros((), jnp.bfloat16))
    outgoing = outgoing.reshape(experts, capacity, width)
    quarter = capacity // narrow_count
    own_rows = lax.dynamic_slice_in_dim(outgoing, lax.axis_index("narrow") * quarter, quarter, 1)
    arrived = lax.all_to_all(own_rows, "wide", split_axis=0, concat_axis=0, tiled=True)
    joined = lax.all_gather(arrived, "narrow", axis=1, tiled=True)
    partial_value = expert_ffn(joined, w_gate, w_up, w_down)
    expert_out = (
        lax.psum_scatter(partial_value, "narrow", scatter_dimension=2, tiled=True)
        .astype(jnp.float32)
        .astype(jnp.bfloat16)
    )
    returned = lax.all_to_all(expert_out, "wide", split_axis=0, concat_axis=0, tiled=True)
    returned_rows = returned.reshape(experts * capacity, returned.shape[2])
    pair_rows = returned_rows[target_slot].astype(jnp.float32)
    weighted = gate_weights.reshape(pairs, 1) * pair_rows
    routed = jnp.sum(weighted.reshape(tok_count, top_count, returned.shape[2]), axis=1)
    gate_sum = jnp.dot(
        tokens,
        lax.all_gather(shared_gate, "wide", axis=0, tiled=True),
        preferred_element_type=jnp.float32,
    )
    up_sum = jnp.dot(
        tokens,
        lax.all_gather(shared_up, "wide", axis=0, tiled=True),
        preferred_element_type=jnp.float32,
    )
    shared_hidden = (jax.nn.silu(gate_sum) * up_sum).astype(jnp.bfloat16)
    shared_terms = jnp.dot(
        shared_hidden,
        lax.all_gather(shared_down, "wide", axis=1, tiled=True),
        preferred_element_type=jnp.float32,
    )
    shared = lax.psum_scatter(shared_terms, "narrow", scatter_dimension=1, tiled=True)
    return (shared + routed).astype(jnp.bfloat16)


MESH = pl.DeviceIdType.MESH
ANY = pl.BlockSpec(memory_space=pl.ANY)
VMEM = pl.BlockSpec(memory_space=pltpu.VMEM)
LANES = 128
PLANE = 4


def plan(tok_count, top_count, experts, wide_count):
    capacity = min(tok_count, 4 * tok_count * top_count // (3 * experts))
    return capacity, wide_count * tok_count <= 4 * experts * capacity


def greet(devices):
    barrier = pltpu.get_barrier_semaphore()
    for device in devices:
        pl.semaphore_signal(barrier, inc=1, device_id=device, device_id_type=MESH)
    pl.semaphore_wait(barrier, len(devices))


def fused_kernel(
    wide,
    slots,
    tok,
    gate,
    up,
    down,
    dense,
    w_gate_in,
    w_up_in,
    w_down_in,
    out,
    every,
    all_gate,
    all_up,
    all_down,
    weight,
    w_gate,
    w_up,
    w_down,
    rows,
    slot_w,
    both,
    other,
    acc,
    twin_in,
    diag_in,
    side_in,
    line_in,
    send,
    recv,
    local,
):
    f32, bf16 = jnp.float32, jnp.bfloat16
    me = lax.axis_index("wide")
    core = lax.axis_index("narrow")
    lines = wide // PLANE
    count = tok.shape[0]
    share = count // 2
    half = share // 2
    pieces = gate.shape[1] // LANES
    greet([(me ^ k, core) for k in range(1, wide)] + [(me, 1 - core)])
    x_peer, y_peer, twin = (me ^ 1, core), (me ^ 2, core), (me, 1 - core)
    started = []

    def pos(k):
        return (k % PLANE) * lines + k // PLANE

    def copy(number, source, target, device):
        return pltpu.make_async_remote_copy(
            src_ref=source,
            dst_ref=target,
            send_sem=send.at[number],
            recv_sem=recv.at[number],
            device_id=device,
            device_id_type=MESH,
        )

    def start(item):
        item.start()
        started.append(item)

    def landed(number, place):
        copy(number, place, place, twin).wait_recv()

    def region(k, side=None, of=core):
        begin = pos(k) * count + of * share
        if side is None:
            return every.at[pl.ds(pl.multiple_of(begin, share), share)]
        return every.at[pl.ds(pl.multiple_of(begin + side * half, half), half)]

    Z, X, Y, XD, YD, T = (lines * i for i in range(6))
    W = T + 5 * lines
    R = W + 4 * wide

    def arrive(number, place):
        landed(number, place)
        start(copy(T + number, place, place, twin))

    own = pltpu.make_async_copy(tok, every.at[pl.ds(0, count)], local.at[0])
    own.start()
    mine = tok.at[pl.ds(pl.multiple_of(core * share, share), share)]
    start(copy(X, mine, region(1), x_peer))
    start(copy(Y, mine, region(2), y_peer))
    for d in range(1, lines):
        start(copy(Z + d, mine, region(PLANE * d), (me ^ (PLANE * d), core)))
    for k in range(1, wide):
        start(copy(W + k, dense.at[me ^ k], weight.at[pos(k)], (me ^ k, core)))
    loads = [pltpu.make_async_copy(dense.at[me], weight.at[0], local.at[1])]
    for number, (source, target) in enumerate(
        ((w_gate_in, w_gate), (w_up_in, w_up), (w_down_in, w_down))
    ):
        loads.append(pltpu.make_async_copy(source, target, local.at[5 + number]))
    for item in loads:
        item.start()

    def shared_copies(k):
        part = pl.ds(pl.multiple_of((me ^ k) * LANES, LANES), LANES)
        place = pl.ds(pl.multiple_of(me * LANES, LANES), LANES)
        to = (me ^ k, core)
        return [
            copy(W + k + wide, gate.at[:, part], all_gate.at[place], to),
            copy(W + k + 2 * wide, up.at[:, part], all_up.at[place], to),
            copy(W + k + 3 * wide, down.at[part], all_down.at[:, place], to),
        ]

    def send_shared(ks):
        for k in ks:

            @pl.when((me ^ k) < pieces)
            def _():
                for item in shared_copies(k):
                    item.start()

    def line(d):
        arrive(Z + d, region(PLANE * d))
        start(copy(X + d, region(PLANE * d), region(PLANE * d ^ 1), x_peer))
        start(copy(Y + d, region(PLANE * d), region(PLANE * d ^ 2), y_peer))

    def beside(d):
        k = 1 ^ (PLANE * d)
        arrive(X + d, region(k))
        start(copy(YD + d, region(k, 1), region(k ^ 2, 1), y_peer))
        k = 2 ^ (PLANE * d)
        arrive(Y + d, region(k))
        start(copy(XD + d, region(k, 0), region(k ^ 1, 0), x_peer))

    send_shared(range(1, wide))
    beside(0)
    for d in range(1, lines):
        line(d)
        if d >= 2:
            beside(d - 1)

    @pl.when(me < pieces)
    def _():
        part = pl.ds(pl.multiple_of(me * LANES, LANES), LANES)
        items = [
            pltpu.make_async_copy(gate.at[:, part], all_gate.at[part], local.at[2]),
            pltpu.make_async_copy(up.at[:, part], all_up.at[part], local.at[3]),
            pltpu.make_async_copy(down.at[part], all_down.at[:, part], local.at[4]),
        ]
        for item in items:
            item.start()
        for item in items:
            item.wait()

    @pl.when(me >= pieces)
    def _():
        all_gate[...] = jnp.zeros_like(all_gate)
        all_up[...] = jnp.zeros_like(all_up)
        all_down[...] = jnp.zeros_like(all_down)

    block = lines * count
    lane_r = lax.broadcasted_iota(jnp.int32, (count, count), 0)
    lane_c = lax.broadcasted_iota(jnp.int32, (count, count), 1)
    upper = (lane_r <= lane_c).astype(f32).astype(bf16)
    slot = lax.broadcasted_iota(jnp.int32, (slots, count), 0).astype(f32)

    def across(a, b):
        return lax.dot_general(a, b, (((1,), (1,)), ((), ())), preferred_element_type=f32)

    def routed_hidden(group):
        picks = []
        for b in range(lines):
            value = weight[group * lines + b]
            chosen = (value > 0.0).astype(f32)
            rank = jnp.dot(chosen.astype(bf16), upper, preferred_element_type=f32)
            where = jnp.where(chosen > 0.0, rank - 1.0, -1.0)[0:1]
            pick = (jnp.broadcast_to(where, (slots, count)) == slot).astype(f32)
            picks.append(pick)
            place = pl.ds(b * slots, slots)
            slot_w[place] = jnp.sum(pick * value[0:1], axis=1, keepdims=True)
            at = pl.ds(pl.multiple_of(group * block + b * count, count), count)
            rows[place] = jnp.dot(
                pick.astype(bf16), every[at], preferred_element_type=f32
            ).astype(bf16)
        gate_part = across(rows[...], w_gate[...])
        up_part = across(rows[...], w_up[...])
        hidden = (jax.nn.silu(gate_part) * up_part * slot_w[...]).astype(bf16)
        for b in range(lines):
            spread = jnp.dot(
                picks[b].T.astype(bf16),
                hidden[b * slots : (b + 1) * slots],
                preferred_element_type=f32,
            )
            at = pl.ds(pl.multiple_of(group * block + b * count, count), count)
            both[at] = spread.astype(bf16)

    width = out.shape[1]

    def finish(group):
        at = pl.ds(pl.multiple_of(group * block, block), block)
        gate_part = jnp.dot(every[at], all_gate[...], preferred_element_type=f32)
        up_part = jnp.dot(every[at], all_up[...], preferred_element_type=f32)
        shared = (jax.nn.silu(gate_part) * up_part).astype(bf16)
        for target, which in ((other, 1 - core), (acc, core)):
            columns = pl.ds(pl.multiple_of(which * width, width), width)
            part = jnp.dot(both[at], w_down[:, columns], preferred_element_type=f32)
            part += jnp.dot(shared, all_down[:, columns], preferred_element_type=f32)
            target[at] = part.astype(bf16)

    for k in range(1, wide):
        landed(W + k, weight.at[pos(k)])
    for item in loads:
        item.wait()
    own.wait()
    for d in range(1, lines):
        landed(T + Z + d, region(PLANE * d, None, 1 - core))
    routed_hidden(0)
    beside(lines - 1)
    for d in range(lines):
        landed(T + X + d, region(PLANE * d ^ 1, None, 1 - core))
        landed(T + Y + d, region(PLANE * d ^ 2, None, 1 - core))

    def early(group, carry):
        routed_hidden(group)
        return carry

    lax.fori_loop(1, 3, early, 0)
    for d in range(lines):
        arrive(XD + d, region(3 ^ (PLANE * d), 0))
        arrive(YD + d, region(3 ^ (PLANE * d), 1))
    for d in range(lines):
        landed(T + XD + d, region(3 ^ (PLANE * d), 0, 1 - core))
        landed(T + YD + d, region(3 ^ (PLANE * d), 1, 1 - core))
    routed_hidden(3)
    for k in range(1, wide):

        @pl.when(me < pieces)
        def _():
            place = pl.ds(pl.multiple_of((me ^ k) * LANES, LANES), LANES)
            places = (all_gate.at[place], all_up.at[place], all_down.at[:, place])
            for number, target in enumerate(places):
                landed(W + k + (number + 1) * wide, target)

    RT, RXD, RYD = R, R + wide, R + wide + lines
    RX, RY, RZ = RYD + lines, RYD + 2 * lines, RYD + 3 * lines
    step = 16

    def rows_of(ref, k, begin=0, size=count):
        return ref.at[pl.ds(pos(k) * count + begin, size)]

    def add(target, sources):
        def one(i, carry):
            at = pl.ds(pl.multiple_of(i * step, step), step)
            value = target[at].astype(f32)
            for source in sources:
                value += source[at].astype(f32)
            target[at] = value.astype(bf16)
            return carry

        lax.fori_loop(0, target.shape[0] // step, one, 0)

    def hand_over(flip):
        finish(flip)
        for d in range(lines):
            k = flip ^ (PLANE * d)
            start(copy(RT + k, rows_of(other, k), rows_of(twin_in, k), twin))

    def fold(k):
        landed(RT + k, rows_of(twin_in, k))
        add(rows_of(acc, k), [rows_of(twin_in, k)])

    order = list(range(lines - 1, 0, -1)) + [0]
    tall = count // 2
    hand_over(3)
    for d in order:
        k = 3 ^ (PLANE * d)
        fold(k)
        start(copy(RXD + d, rows_of(acc, k, 0, tall), diag_in.at[0, d], x_peer))
        start(copy(RYD + d, rows_of(acc, k, tall, tall), diag_in.at[1, d], y_peer))
    hand_over(2)
    hand_over(1)
    for d in order:
        k = 2 ^ (PLANE * d)
        fold(k)
        landed(RXD + d, diag_in.at[0, d])
        add(rows_of(acc, k, 0, tall), [diag_in.at[0, d]])
        start(copy(RY + d, rows_of(acc, k), side_in.at[1, d], y_peer))
        k = 1 ^ (PLANE * d)
        fold(k)
        landed(RYD + d, diag_in.at[1, d])
        add(rows_of(acc, k, tall, tall), [diag_in.at[1, d]])
        start(copy(RX + d, rows_of(acc, k), side_in.at[0, d], x_peer))
    hand_over(0)
    for d in order:
        fold(PLANE * d)
    for d in order:
        k = PLANE * d
        landed(RX + d, side_in.at[0, d])
        landed(RY + d, side_in.at[1, d])
        if d > 0:
            add(rows_of(acc, k), [side_in.at[0, d], side_in.at[1, d]])
            start(copy(RZ + d, rows_of(acc, k), line_in.at[d], (me ^ k, core)))
    for d in range(1, lines):
        landed(RZ + d, line_in.at[d])

    def last(i, carry):
        at = pl.ds(pl.multiple_of(i * step, step), step)
        value = acc[at].astype(f32)
        value += side_in[0, 0, at].astype(f32) + side_in[1, 0, at].astype(f32)
        for d in range(1, lines):
            value += line_in[d, at].astype(f32)
        out[at] = value.astype(bf16)
        return carry

    lax.fori_loop(0, count // step, last, 0)
    for k in range(1, wide):

        @pl.when((me ^ k) < pieces)
        def _():
            for item in shared_copies(k):
                item.wait_send()

    for item in started:
        item.wait_send()


def fused(wide, narrow, slots, tokens, gate, up, down, dense, w_gate, w_up, w_down):
    count, width = tokens.shape
    part = width // narrow
    lines = wide // PLANE
    total = wide * count
    sems = 10 * lines + 4 * wide + wide + 5 * lines
    bf16, f32 = jnp.bfloat16, jnp.float32
    return pl.pallas_call(
        functools.partial(fused_kernel, wide, slots),
        out_shape=jax.ShapeDtypeStruct((count, part), bf16),
        in_specs=[VMEM] * 5 + [ANY] * 3,
        out_specs=VMEM,
        scratch_shapes=[
            pltpu.VMEM((total, width), bf16),
            pltpu.VMEM((wide * gate.shape[0], LANES), bf16),
            pltpu.VMEM((wide * gate.shape[0], LANES), bf16),
            pltpu.VMEM((LANES, wide * down.shape[1]), bf16),
            pltpu.VMEM((wide, 8, count), f32),
            pltpu.VMEM(w_gate.shape, bf16),
            pltpu.VMEM(w_up.shape, bf16),
            pltpu.VMEM(w_down.shape, bf16),
            pltpu.VMEM((lines * slots, width), bf16),
            pltpu.VMEM((lines * slots, 1), f32),
            pltpu.VMEM((total, w_gate.shape[0]), bf16),
            pltpu.VMEM((total, part), bf16),
            pltpu.VMEM((total, part), bf16),
            pltpu.VMEM((total, part), bf16),
            pltpu.VMEM((2, lines, count // 2, part), bf16),
            pltpu.VMEM((2, lines, count, part), bf16),
            pltpu.VMEM((lines, count, part), bf16),
            pltpu.SemaphoreType.DMA((sems,)),
            pltpu.SemaphoreType.DMA((sems,)),
            pltpu.SemaphoreType.DMA((8,)),
        ],
        compiler_params=pltpu.CompilerParams(
            collective_id=0, has_side_effects=True, vmem_limit_bytes=63 << 20
        ),
    )(tokens, gate, up, down, dense, w_gate, w_up, w_down)


def gather_body(
    tokens,
    expert_ids,
    gate_weights,
    shared_gate,
    shared_up,
    shared_down,
    expert_gate,
    expert_up,
    expert_down,
):
    tok_count, top_count = expert_ids.shape
    wide = lax.axis_size("wide")
    narrow = lax.axis_size("narrow")
    experts = wide * expert_gate.shape[0]
    capacity, _ = plan(tok_count, top_count, experts, wide)
    names = jnp.arange(experts, dtype=jnp.int32)
    match = expert_ids.T[None, :, :] == names[:, None, None]
    dense = jnp.sum(jnp.where(match, gate_weights.T[None, :, :], 0.0), axis=1)
    dense = jnp.broadcast_to(dense[:, None, :], (experts, 8, tok_count))
    return fused(
        wide,
        narrow,
        capacity,
        tokens,
        shared_gate,
        shared_up,
        shared_down,
        dense,
        expert_gate[0].T,
        expert_up[0].T,
        expert_down[0],
    )


def solution(mesh):
    in_specs = (
        P("wide", None),
        P("wide", None),
        P("wide", None),
        P("wide", "narrow"),
        P("wide", "narrow"),
        P("narrow", "wide"),
        P("wide", None, "narrow"),
        P("wide", None, "narrow"),
        P("wide", "narrow", None),
    )
    out_specs = P("wide", "narrow")
    wide_count = mesh.shape["wide"]

    def body(*args):
        tok_count, top_count = args[1].shape
        gathers = plan(tok_count, top_count, wide_count * args[6].shape[0], wide_count)[1]
        return (gather_body if gathers else dispatch_body)(*args)

    return jax.shard_map(body, mesh=mesh, in_specs=in_specs, out_specs=out_specs, check_vma=False)
```

profile of v0, /device:TPU:0, one launch (start us, length us, event | category | flops | bytes accessed | tf_op | source)
XLA Modules:
  0.0 119.4 jit_solution(8871451005376386091)
XLA Ops:
  0.0 0.7 select_reduce_fusion
  0.7 0.6 broadcast_in_dim.23.dense
  1.4 116.3 %shard_map.91 = bf16[128,1024]{1,0:T(8,128)(2,1)} custom-call(bf16[128,2048]{1,0:T(8,128)(2,1)} %tok.1, bf16[128,1408]{1,0:T(8,128)(2,1)} %gate.1, bf16[128,1408]{1,0:T(8,128)(2,1)} %up.1, bf16[1408,128]{1,0:T(8,128)(2,1)} %down.1, f32[16,8,128]{2,1,0:T(8,128)} %broadcast_in_dim.23.dense, bf16[704,2048]{1,0:T(8,128)(2,1)} %bitcast.9, ...), custom_call_target="tpu_custom_call" | custom-call | tf_op jit(solution)/shard_map/pallas_call | solution.py:435
  117.7 1.7 %copy.11 = bf16[128,1024]{1,0:T(8,128)(2,1)} copy(bf16[128,1024]{1,0:T(8,128)(2,1)} %shard_map.91) | data formatting | bytes 524288
where the time goes:
time: 121 us; the launch traced here: 119 us
  Pallas kernels  116 us (96%)
  local copies, waits for them, and re-layouts  2.3 us (2%)
    pallas_call x1, Pallas kernels, fused(): pl.pallas_call(functools.partial(fused_kernel, wide, slots), out_shape=ja...  116 us

commit v1 on v0

v1 whole, which is shorter than its diff:
```python
import functools

import jax
import jax.numpy as jnp
from jax import lax
from jax.experimental import pallas as pl
from jax.experimental.pallas import tpu as pltpu
from jax.sharding import PartitionSpec as P


def expert_ffn(received, w_gate, w_up, w_down):
    senders, items, width = received.shape
    flat_rows = received.reshape(senders * items, width)
    gate_part = jnp.dot(flat_rows, w_gate, preferred_element_type=jnp.float32)
    up_part = jnp.dot(flat_rows, w_up, preferred_element_type=jnp.float32)
    hidden = (jax.nn.silu(gate_part) * up_part).astype(jnp.bfloat16)
    partial_value = jnp.dot(hidden, w_down, preferred_element_type=jnp.float32).astype(jnp.bfloat16)
    return partial_value.reshape(senders, items, w_down.shape[1])


def dispatch_body(
    tokens,
    expert_ids,
    gate_weights,
    shared_gate,
    shared_up,
    shared_down,
    expert_gate,
    expert_up,
    expert_down,
):
    tok_count, width = tokens.shape
    top_count = expert_ids.shape[1]
    experts = lax.axis_size("wide") * expert_gate.shape[0]
    capacity = min(tok_count, 4 * tok_count * top_count // (3 * experts))
    narrow_count = lax.axis_size("narrow")
    w_gate = expert_gate[0]
    w_up = expert_up[0]
    w_down = expert_down[0]
    pairs = tok_count * top_count
    flat_ids = expert_ids.reshape(pairs)
    onehot = (flat_ids[:, None] == jnp.arange(experts, dtype=jnp.int32)[None, :]).astype(jnp.int32)
    before = jnp.cumsum(onehot, axis=0) - onehot
    slot_pos = jnp.sum(before * onehot, axis=1)
    target_slot = flat_ids * capacity + slot_pos
    source = (
        jnp.full((experts * capacity,), -1, jnp.int32)
        .at[target_slot]
        .set(jnp.arange(pairs, dtype=jnp.int32))
    )
    filled = source >= 0
    token_of = jnp.where(filled, source // top_count, 0)
    outgoing = jnp.where(filled[:, None], tokens[token_of], jnp.zeros((), jnp.bfloat16))
    outgoing = outgoing.reshape(experts, capacity, width)
    quarter = capacity // narrow_count
    own_rows = lax.dynamic_slice_in_dim(outgoing, lax.axis_index("narrow") * quarter, quarter, 1)
    arrived = lax.all_to_all(own_rows, "wide", split_axis=0, concat_axis=0, tiled=True)
    joined = lax.all_gather(arrived, "narrow", axis=1, tiled=True)
    partial_value = expert_ffn(joined, w_gate, w_up, w_down)
    expert_out = (
        lax.psum_scatter(partial_value, "narrow", scatter_dimension=2, tiled=True)
        .astype(jnp.float32)
        .astype(jnp.bfloat16)
    )
    returned = lax.all_to_all(expert_out, "wide", split_axis=0, concat_axis=0, tiled=True)
    returned_rows = returned.reshape(experts * capacity, returned.shape[2])
    pair_rows = returned_rows[target_slot].astype(jnp.float32)
    weighted = gate_weights.reshape(pairs, 1) * pair_rows
    routed = jnp.sum(weighted.reshape(tok_count, top_count, returned.shape[2]), axis=1)
    gate_sum = jnp.dot(
        tokens,
        lax.all_gather(shared_gate, "wide", axis=0, tiled=True),
        preferred_element_type=jnp.float32,
    )
    up_sum = jnp.dot(
        tokens,
        lax.all_gather(shared_up, "wide", axis=0, tiled=True),
        preferred_element_type=jnp.float32,
    )
    shared_hidden = (jax.nn.silu(gate_sum) * up_sum).astype(jnp.bfloat16)
    shared_terms = jnp.dot(
        shared_hidden,
        lax.all_gather(shared_down, "wide", axis=1, tiled=True),
        preferred_element_type=jnp.float32,
    )
    shared = lax.psum_scatter(shared_terms, "narrow", scatter_dimension=1, tiled=True)
    return (shared + routed).astype(jnp.bfloat16)


MESH = pl.DeviceIdType.MESH
ANY = pl.BlockSpec(memory_space=pl.ANY)
VMEM = pl.BlockSpec(memory_space=pltpu.VMEM)
LANES = 128
PLANE = 4


def plan(tok_count, top_count, experts, wide_count):
    capacity = min(tok_count, 4 * tok_count * top_count // (3 * experts))
    return capacity, wide_count == PLANE**2 and wide_count * tok_count <= 4 * experts * capacity


def homes(wide, pieces, core):
    lines = wide // PLANE
    order = []
    for turn in range(PLANE):
        for z in range(lines):
            spot = (turn, PLANE - 1 - turn)[(z + core) % 2]
            order.append(PLANE * (z if core else lines - 1 - z) + spot)
    return order[:pieces]


def piece_table(wide, pieces, core, chip):
    bits = pieces.bit_length()
    per = 30 // bits
    words = []
    for which in range(2):
        held = homes(wide, pieces, which)
        row = [held.index(j) if j in held else pieces for j in range(wide)]
        words.append(
            [
                sum(v << (bits * i) for i, v in enumerate(row[at : at + per]))
                for at in range(0, wide, per)
            ]
        )
    word = jnp.int32(0)
    for i, (low, high) in enumerate(zip(*words)):
        word = jnp.where(chip // per == i, jnp.where(core == 0, low, high), word)
    return (word >> (bits * (chip % per))) & ((1 << bits) - 1)


def greet(devices):
    barrier = pltpu.get_barrier_semaphore()
    for device in devices:
        pl.semaphore_signal(barrier, inc=1, device_id=device, device_id_type=MESH)
    pl.semaphore_wait(barrier, len(devices))


def fused_kernel(
    wide,
    slots,
    tok,
    ids,
    gains,
    gate,
    up,
    down,
    w_gate_in,
    w_up_in,
    w_down_in,
    out,
    every,
    all_in,
    all_ids,
    all_gains,
    w_gate,
    w_up,
    w_out,
    rows,
    slot_w,
    both,
    other,
    acc,
    twin_in,
    diag_in,
    side_in,
    line_in,
    send,
    recv,
    local,
):
    f32, bf16 = jnp.float32, jnp.bfloat16
    me = lax.axis_index("wide")
    core = lax.axis_index("narrow")
    lines = wide // PLANE
    count = tok.shape[0]
    share = count // 2
    half = share // 2
    pieces = gate.shape[1] // LANES
    my_piece = piece_table(wide, pieces, core, me)
    greet([(me ^ k, core) for k in range(1, wide)] + [(me, 1 - core)])
    x_peer, y_peer, twin = (me ^ 1, core), (me ^ 2, core), (me, 1 - core)
    plane = me // PLANE
    inner = (plane > 0) & (plane < lines - 1)
    started = []
    inner_started = []
    outer_started = []

    def copy(number, source, target, device, sent=None):
        return pltpu.make_async_remote_copy(
            src_ref=source,
            dst_ref=target,
            send_sem=send.at[number if sent is None else sent],
            recv_sem=recv.at[number],
            device_id=device,
            device_id_type=MESH,
        )

    def start(item):
        item.start()
        started.append(item)

    def start_inner(item):
        inner_started.append(item)

        @pl.when(inner)
        def _():
            item.start()

    def landed(number, place):
        copy(number, place, place, twin).wait_recv()

    def region(k, side=None, of=core):
        begin = k * count + of * share
        if side is None:
            return every.at[pl.ds(pl.multiple_of(begin, share), share)]
        return every.at[pl.ds(pl.multiple_of(begin + side * half, half), half)]

    Z, X, Y, XD, YD, T = (lines * i for i in range(6))
    W = T + 5 * lines
    G = W + 3 * wide
    R = G + 2 * wide
    E = R + wide + 4 * lines + 5

    def arrive(number, place):
        landed(number, place)
        start(copy(T + number, place, place, twin))

    def joined(number, k, side=None):
        landed(T + number, region(k, side, 1 - core))

    own = pltpu.make_async_copy(tok, every.at[pl.ds(0, count)], local.at[0])
    own.start()
    mine = tok.at[pl.ds(pl.multiple_of(core * share, share), share)]
    near, far = (me ^ PLANE, core), (me ^ (3 * PLANE), core)
    start(copy(X, mine, region(1), x_peer))
    start(copy(Y, mine, region(2), y_peer))
    start(copy(Z + 1, mine, region(PLANE), near))
    start_inner(copy(Z + 3, mine, region(3 * PLANE), far, E))
    for k in range(1, wide):
        start(copy(G + k, ids, all_ids.at[k], (me ^ k, core)))
        start(copy(G + wide + k, gains, all_gains.at[k], (me ^ k, core)))
    loads = [
        pltpu.make_async_copy(ids, all_ids.at[0], local.at[1]),
        pltpu.make_async_copy(gains, all_gains.at[0], local.at[8]),
    ]
    w_down = w_out.at[pl.ds(LANES, w_down_in.shape[0])]
    for number, (source, target) in enumerate(
        ((w_gate_in, w_gate), (w_up_in, w_up), (w_down_in, w_down))
    ):
        loads.append(pltpu.make_async_copy(source, target, local.at[5 + number]))
    for item in loads:
        item.start()

    def places(chip):
        at = pl.ds(pl.multiple_of(chip * LANES, LANES), LANES)
        return (
            all_in.at[at, pl.ds(0, LANES)],
            all_in.at[at, pl.ds(LANES, LANES)],
            w_out.at[pl.ds(0, LANES), at],
        )

    def parts(piece):
        piece = jnp.minimum(piece, pieces - 1)
        part = pl.ds(pl.multiple_of(piece * LANES, LANES), LANES)
        return (gate.at[:, part], up.at[:, part], down.at[part])

    def shared_copies(k):
        piece = piece_table(wide, pieces, core, me ^ k)
        return [
            copy(W + k + i * wide, source, target, (me ^ k, core))
            for i, (source, target) in enumerate(zip(parts(piece), places(me)))
        ]

    def send_shared(ks):
        for k in ks:

            @pl.when(piece_table(wide, pieces, core, me ^ k) < pieces)
            def _():
                for item in shared_copies(k):
                    item.start()

    def stage(d):
        landed(Z + d, region(PLANE * d))

    def spread(d):
        place = region(PLANE * d)
        start(copy(X + d, place, region((PLANE * d) ^ 1), x_peer))
        start(copy(Y + d, place, region((PLANE * d) ^ 2), y_peer))
        start(copy(T + Z + d, place, place, twin))

    def spread_if(where, d):
        place = region(PLANE * d)
        items = [
            copy(X + d, place, region((PLANE * d) ^ 1), x_peer),
            copy(Y + d, place, region((PLANE * d) ^ 2), y_peer),
            copy(T + Z + d, place, place, twin),
        ]

        @pl.when(where)
        def _():
            for item in items:
                item.start()

    def beside(d):
        k = 1 ^ (PLANE * d)
        arrive(X + d, region(k))
        start(copy(YD + d, region(k, 1), region(k ^ 2, 1), y_peer))
        k = 2 ^ (PLANE * d)
        arrive(Y + d, region(k))
        start(copy(XD + d, region(k, 0), region(k ^ 1, 0), x_peer))

    def corner(d):
        k = 3 ^ (PLANE * d)
        arrive(XD + d, region(k, 0))
        arrive(YD + d, region(k, 1))

    lane_r = lax.broadcasted_iota(jnp.int32, (count, count), 0)
    lane_c = lax.broadcasted_iota(jnp.int32, (count, count), 1)
    upper = (lane_r <= lane_c).astype(f32).astype(bf16)
    slot = lax.broadcasted_iota(jnp.int32, (slots, count), 0).astype(f32)

    def across(a, b):
        return lax.dot_general(a, b, (((1,), (1,)), ((), ())), preferred_element_type=f32)

    def block(k):
        return pl.ds(pl.multiple_of(k * count, count), count)

    def routed(ks):
        picks = []
        for b, k in enumerate(ks):
            match = all_ids[k] == me
            value = jnp.sum(jnp.where(match, all_gains[k], 0.0), axis=0, keepdims=True)
            chosen = jnp.sum(match.astype(f32), axis=0, keepdims=True)
            chosen = jnp.broadcast_to(chosen, (8, count))
            rank = jnp.dot(chosen.astype(bf16), upper, preferred_element_type=f32)
            where = jnp.where(chosen > 0.0, rank - 1.0, -1.0)[0:1]
            pick = (jnp.broadcast_to(where, (slots, count)) == slot).astype(f32)
            picks.append(pick)
            place = pl.ds(b * slots, slots)
            slot_w[place] = jnp.sum(pick * value, axis=1, keepdims=True)
            rows[place] = jnp.dot(
                pick.astype(bf16), every[block(k)], preferred_element_type=f32
            ).astype(bf16)
        gate_part = across(rows[...], w_gate[...])
        up_part = across(rows[...], w_up[...])
        hidden = (jax.nn.silu(gate_part) * up_part * slot_w[...]).astype(bf16)
        for b, k in enumerate(ks):
            back = jnp.dot(
                picks[b].T.astype(bf16),
                hidden[b * slots : (b + 1) * slots],
                preferred_element_type=f32,
            )
            both[block(k), LANES:] = back.astype(bf16)

    width = out.shape[1]

    def partials(at):
        pre = jnp.dot(every[at], all_in[...], preferred_element_type=f32)
        both[at, :LANES] = (jax.nn.silu(pre[:, :LANES]) * pre[:, LANES:]).astype(bf16)
        for target, which in ((other, 1 - core), (acc, core)):
            columns = pl.ds(pl.multiple_of(which * width, width), width)
            part = jnp.dot(both[at], w_out[:, columns], preferred_element_type=f32)
            target[at] = part.astype(bf16)

    second = jnp.where(inner, 3, 2)
    third = 5 - second
    EARLY, MIDDLE = [], [12, 8, 13, 9, 14, 10, 15, 11]
    send_shared(EARLY)

    @pl.when(my_piece < pieces)
    def _():
        items = [
            pltpu.make_async_copy(source, target, local.at[2 + i])
            for i, (source, target) in enumerate(zip(parts(my_piece), places(me)))
        ]
        for item in items:
            item.start()
        for item in items:
            item.wait()

    @pl.when(my_piece >= pieces)
    def _():
        all_in[...] = jnp.zeros_like(all_in)
        w_out[0:LANES] = jnp.zeros((LANES, w_out.shape[1]), bf16)

    stage(1)
    start_inner(copy(Z + 2, region(PLANE), region(2 * PLANE), far, E + 1))
    spread(1)

    @pl.when(inner)
    def _():
        stage(3)
        copy(Z + 2, region(3 * PLANE), region(2 * PLANE), near, E + 2).start()

    spread_if(inner, 3)
    beside(0)
    for k in range(1, wide):
        landed(G + k, all_ids.at[k])
        landed(G + wide + k, all_gains.at[k])
    for item in loads:
        item.wait()
    own.wait()
    joined(Z + 1, PLANE)
    joined(X, 1)
    joined(Y, 2)
    routed([0, 1, 2, PLANE])

    @pl.when(jnp.logical_not(inner))
    def _():
        stage(2)

    spread_if(jnp.logical_not(inner), 2)
    beside(1)
    stage(third)
    start_inner(copy(Z + 3, region(2 * PLANE), region(3 * PLANE), near, E + 3))
    spread(third)
    send_shared(MIDDLE)
    corner(0)
    joined(Z + second, PLANE * second)
    joined(X + 1, PLANE ^ 1)
    joined(Y + 1, PLANE ^ 2)
    joined(XD, 3, 0)
    joined(YD, 3, 1)
    routed([PLANE * second, PLANE ^ 1, PLANE ^ 2, 3])
    beside(second)
    beside(third)
    send_shared([k for k in range(1, wide) if k not in EARLY + MIDDLE])
    corner(1)
    joined(Z + third, PLANE * third)
    joined(X + second, (PLANE * second) ^ 1)
    joined(Y + second, (PLANE * second) ^ 2)
    joined(XD + 1, 3 ^ PLANE, 0)
    joined(YD + 1, 3 ^ PLANE, 1)
    routed([PLANE * third, (PLANE * second) ^ 1, (PLANE * second) ^ 2, 3 ^ PLANE])
    corner(second)
    corner(third)
    joined(X + third, (PLANE * third) ^ 1)
    joined(Y + third, (PLANE * third) ^ 2)
    for d in (second, third):
        joined(XD + d, 3 ^ (PLANE * d), 0)
        joined(YD + d, 3 ^ (PLANE * d), 1)
    routed(
        [
            (PLANE * third) ^ 1,
            (PLANE * third) ^ 2,
            3 ^ (PLANE * second),
            3 ^ (PLANE * third),
        ]
    )
    for k in range(1, wide):

        @pl.when(my_piece < pieces)
        def _():
            for i, target in enumerate(places(me ^ k)):
                landed(W + k + i * wide, target)

    RT, RXD, RYD = R, R + wide, R + wide + lines
    RX, RY, RZ = RYD + lines, RYD + 2 * lines, RYD + 3 * lines
    step = 16

    def rows_of(ref, k, begin=0, size=count):
        return ref.at[pl.ds(k * count + begin, size)]

    def add(target, sources):
        def one(i, carry):
            at = pl.ds(pl.multiple_of(i * step, step), step)
            value = target[at].astype(f32)
            for source in sources:
                value += source[at].astype(f32)
            target[at] = value.astype(bf16)
            return carry

        lax.fori_loop(0, target.shape[0] // step, one, 0)

    def compute(d, flips):
        first = PLANE * d + flips[0]
        partials(pl.ds(first * count, len(flips) * count))
        for flip in flips:
            k = PLANE * d + flip
            start(copy(RT + k, rows_of(other, k), rows_of(twin_in, k), twin))

    def fold(k):
        landed(RT + k, rows_of(twin_in, k))
        add(rows_of(acc, k), [rows_of(twin_in, k)])

    tall = count // 2

    def diagonal(d):
        k = 3 ^ (PLANE * d)
        fold(k)
        start(copy(RXD + d, rows_of(acc, k, 0, tall), diag_in.at[0, d], x_peer))
        start(copy(RYD + d, rows_of(acc, k, tall, tall), diag_in.at[1, d], y_peer))

    def sides(d):
        k = 2 ^ (PLANE * d)
        fold(k)
        landed(RXD + d, diag_in.at[0, d])
        add(rows_of(acc, k, 0, tall), [diag_in.at[0, d]])
        start(copy(RY + d, rows_of(acc, k), side_in.at[1, d], y_peer))
        k = 1 ^ (PLANE * d)
        fold(k)
        landed(RYD + d, diag_in.at[1, d])
        add(rows_of(acc, k, tall, tall), [diag_in.at[1, d]])
        start(copy(RX + d, rows_of(acc, k), side_in.at[0, d], x_peer))

    near_in, far_in, far_out = line_in.at[0], line_in.at[1], line_in.at[2]

    def upright(d):
        k = PLANE * d
        fold(k)
        landed(RX + d, side_in.at[0, d])
        landed(RY + d, side_in.at[1, d])
        add(rows_of(acc, k), [side_in.at[0, d], side_in.at[1, d]])

    def outward(number, k, place):
        item = copy(RZ + number, rows_of(acc, k), place, near)
        outer_started.append(item)

        @pl.when(jnp.logical_not(inner))
        def _():
            item.start()

    def inward(number, place, k, item):
        inner_started.append(item)

        @pl.when(inner)
        def _():
            landed(RZ + number, place)
            add(rows_of(acc, k), [place])
            item.start()

    one, two, three = PLANE, 2 * PLANE, 3 * PLANE
    compute(3, [3])
    compute(2, [3])
    diagonal(3)
    compute(3, [1, 2])
    diagonal(2)
    compute(3, [0])
    compute(1, [3])
    sides(3)
    diagonal(1)
    compute(2, [1, 2])
    compute(2, [0])
    sides(2)
    upright(3)
    outward(0, three, near_in)
    compute(0, [3])
    diagonal(0)
    compute(1, [1, 2])
    sides(1)
    compute(1, [0])
    upright(2)
    outward(1, two, far_in)
    inward(0, near_in, two, copy(RZ + 2, rows_of(acc, two), far_out, far))
    compute(0, [1, 2])
    sides(0)
    compute(0, [0])
    inward(1, far_in, three, copy(RZ + 3, rows_of(acc, three), line_in.at[3], far))
    upright(1)
    outward(4, one, line_in.at[4])
    inward(2, far_out, one, copy(RZ + 4, rows_of(acc, one), line_in.at[4], near))
    upright(0)

    @pl.when(inner)
    def _():
        landed(RZ + 3, line_in.at[3])
        add(rows_of(acc, 0), [line_in.at[3]])

    landed(RZ + 4, line_in.at[4])

    def last(i, carry):
        at = pl.ds(pl.multiple_of(i * step, step), step)
        value = acc[at].astype(f32)
        out[at] = (value + line_in[4, at].astype(f32)).astype(bf16)
        return carry

    lax.fori_loop(0, count // step, last, 0)
    for k in range(1, wide):

        @pl.when(piece_table(wide, pieces, core, me ^ k) < pieces)
        def _():
            for item in shared_copies(k):
                item.wait_send()

    for item in started:
        item.wait_send()

    place = region(PLANE * second)
    copy(X + second, place, region((PLANE * second) ^ 1), x_peer).wait_send()
    copy(Y + second, place, region((PLANE * second) ^ 2), y_peer).wait_send()
    copy(T + Z + second, place, place, twin).wait_send()

    @pl.when(inner)
    def _():
        copy(Z + 2, region(3 * PLANE), region(2 * PLANE), near, E + 2).wait_send()
        for item in inner_started:
            item.wait_send()

    @pl.when(jnp.logical_not(inner))
    def _():
        for item in outer_started:
            item.wait_send()


def fused(wide, narrow, slots, tokens, ids, gains, gate, up, down, w_gate, w_up, w_down):
    count, width = tokens.shape
    part = width // narrow
    lines = wide // PLANE
    total = wide * count
    sems = 10 * lines + 6 * wide + 4 * lines + 5 + 4
    bf16, f32 = jnp.bfloat16, jnp.float32
    return pl.pallas_call(
        functools.partial(fused_kernel, wide, slots),
        out_shape=jax.ShapeDtypeStruct((count, part), bf16),
        in_specs=[VMEM] * 6 + [ANY] * 3,
        out_specs=VMEM,
        scratch_shapes=[
            pltpu.VMEM((total, width), bf16),
            pltpu.VMEM((wide * gate.shape[0], 2 * LANES), bf16),
            pltpu.VMEM((wide,) + ids.shape, jnp.int32),
            pltpu.VMEM((wide,) + gains.shape, f32),
            pltpu.VMEM(w_gate.shape, bf16),
            pltpu.VMEM(w_up.shape, bf16),
            pltpu.VMEM((LANES + w_down.shape[0], w_down.shape[1]), bf16),
            pltpu.VMEM((lines * slots, width), bf16),
            pltpu.VMEM((lines * slots, 1), f32),
            pltpu.VMEM((total, LANES + w_gate.shape[0]), bf16),
            pltpu.VMEM((total, part), bf16),
            pltpu.VMEM((total, part), bf16),
            pltpu.VMEM((total, part), bf16),
            pltpu.VMEM((2, lines, count // 2, part), bf16),
            pltpu.VMEM((2, lines, count, part), bf16),
            pltpu.VMEM((5, count, part), bf16),
            pltpu.SemaphoreType.DMA((sems,)),
            pltpu.SemaphoreType.DMA((sems,)),
            pltpu.SemaphoreType.DMA((9,)),
        ],
        compiler_params=pltpu.CompilerParams(
            collective_id=0, has_side_effects=True, vmem_limit_bytes=63 << 20
        ),
    )(tokens, ids, gains, gate, up, down, w_gate, w_up, w_down)


def gather_body(
    tokens,
    expert_ids,
    gate_weights,
    shared_gate,
    shared_up,
    shared_down,
    expert_gate,
    expert_up,
    expert_down,
):
    tok_count, top_count = expert_ids.shape
    wide = lax.axis_size("wide")
    narrow = lax.axis_size("narrow")
    experts = wide * expert_gate.shape[0]
    capacity, _ = plan(tok_count, top_count, experts, wide)
    return fused(
        wide,
        narrow,
        capacity,
        tokens,
        expert_ids.T,
        gate_weights.T,
        shared_gate,
        shared_up,
        shared_down,
        expert_gate[0].T,
        expert_up[0].T,
        expert_down[0],
    )


def solution(mesh):
    in_specs = (
        P("wide", None),
        P("wide", None),
        P("wide", None),
        P("wide", "narrow"),
        P("wide", "narrow"),
        P("narrow", "wide"),
        P("wide", None, "narrow"),
        P("wide", None, "narrow"),
        P("wide", "narrow", None),
    )
    out_specs = P("wide", "narrow")
    wide_count = mesh.shape["wide"]

    def body(*args):
        tok_count, top_count = args[1].shape
        gathers = plan(tok_count, top_count, wide_count * args[6].shape[0], wide_count)[1]
        return (gather_body if gathers else dispatch_body)(*args)

    return jax.shard_map(body, mesh=mesh, in_specs=in_specs, out_specs=out_specs, check_vma=False)
```

time: 121 us -> 110 us (0.909); the launches traced: 119 us -> 110 us
  Pallas kernels: 116 us -> 108 us
    pallas_call x1, Pallas kernels: 116 us -> 108 us  [fused(): pl.pallas_call(functools.partial(fused_kernel, wide, slots), out_shape=ja...]
where the time goes in v1:
time: 110 us
  Pallas kernels  108 us (98%)
  local copies, waits for them, and re-layouts  1.67 us (2%)
    pallas_call x1, Pallas kernels, fused(): pl.pallas_call(functools.partial(fused_kernel, wide, slots), out_shape=ja...  108 us

profile of v1, /device:TPU:0, one launch (start us, length us, event | category | flops | bytes accessed | tf_op | source)
XLA Modules:
  0.0 109.8 jit_solution(2642175660993417917)
XLA Ops:
  0.0 108.1 %shard_map.91 = bf16[128,1024]{1,0:T(8,128)(2,1)} custom-call(bf16[128,2048]{1,0:T(8,128)(2,1)} %tok.1, s32[6,128]{1,0:T(8,128)} %bitcast.12, f32[6,128]{1,0:T(8,128)} %bitcast.13, bf16[128,1408]{1,0:T(8,128)(2,1)} %gate.1, bf16[128,1408]{1,0:T(8,128)(2,1)} %up.1, bf16[1408,128]{1,0:T(8,128)(2,1)} %down.1, bf16[704,2048]{1,0:T(8,128)(2,1)} %bitcast.9, ...), custom_call_target="tpu_custom_call" | custom-call | tf_op jit(solution)/shard_map/pallas_call | solution.py:612
  108.1 1.7 %copy.11 = bf16[128,1024]{1,0:T(8,128)(2,1)} copy(bf16[128,1024]{1,0:T(8,128)(2,1)} %shard_map.91) | data formatting | bytes 524288

commit v2 on v1

--- a/solution.py
+++ b/solution.py
@@ -101,12 +101,17 @@
 
 def homes(wide, pieces, core):
     lines = wide // PLANE
-    order = []
-    for turn in range(PLANE):
-        for z in range(lines):
-            spot = (turn, PLANE - 1 - turn)[(z + core) % 2]
-            order.append(PLANE * (z if core else lines - 1 - z) + spot)
-    return order[:pieces]
+    inner, edge, late = [], [], []
+    for z in range(lines):
+        pair = [PLANE * z + i for i in ((1, 2) if z % 2 else (0, 3))]
+        if 0 < z < lines - 1:
+            inner += pair
+        else:
+            edge.append(pair[0])
+            late.append(pair[1])
+    both = (inner + edge + late)[: max(0, 2 * pieces - wide)]
+    single = [chip for chip in range(wide) if chip not in both]
+    return (both + single[core::2])[:pieces]
 
 
 def piece_table(wide, pieces, core, chip):
@@ -164,6 +169,7 @@
     diag_in,
     side_in,
     line_in,
+    plane_in,
     send,
     recv,
     local,
@@ -209,33 +215,40 @@
     def landed(number, place):
         copy(number, place, place, twin).wait_recv()
 
-    def region(k, side=None, of=core):
-        begin = k * count + of * share
-        if side is None:
-            return every.at[pl.ds(pl.multiple_of(begin, share), share)]
-        return every.at[pl.ds(pl.multiple_of(begin + side * half, half), half)]
-
-    Z, X, Y, XD, YD, T = (lines * i for i in range(6))
-    W = T + 5 * lines
+    def region(k, side=None, of=core, begin=0, size=None):
+        first = k * count + of * share
+        if size is not None:
+            first, tile, size = first + begin, LANES // 8, size
+        elif side is None:
+            tile = size = share
+        else:
+            first, tile, size = first + side * half, half, half
+        return every.at[pl.ds(pl.multiple_of(first, tile), size)]
+
+    Z, X, Y, XD, YD, B = 0, 2 * lines, 4 * lines, 6 * lines, 7 * lines, 8 * lines
+    T = 9 * lines
+    W = 2 * T
     G = W + 3 * wide
     R = G + 2 * wide
-    E = R + wide + 4 * lines + 5
+    RC = R + wide + 4 * lines
+    E = RC + 10 + 9
 
     def arrive(number, place):
         landed(number, place)
         start(copy(T + number, place, place, twin))
 
-    def joined(number, k, side=None):
-        landed(T + number, region(k, side, 1 - core))
+    def joined(number, place):
+        landed(T + number, place)
 
     own = pltpu.make_async_copy(tok, every.at[pl.ds(0, count)], local.at[0])
     own.start()
-    mine = tok.at[pl.ds(pl.multiple_of(core * share, share), share)]
     near, far = (me ^ PLANE, core), (me ^ (3 * PLANE), core)
-    start(copy(X, mine, region(1), x_peer))
-    start(copy(Y, mine, region(2), y_peer))
-    start(copy(Z + 1, mine, region(PLANE), near))
-    start_inner(copy(Z + 3, mine, region(3 * PLANE), far, E))
+    for h in range(2):
+        mine = tok.at[pl.ds(pl.multiple_of(core * share + h * half, half), half)]
+        start(copy(Z + 2 + h, mine, region(PLANE, h), near))
+        start_inner(copy(Z + 6 + h, mine, region(3 * PLANE, h), far, E + h))
+        start(copy(X + h, mine, region(1, h), x_peer))
+        start(copy(Y + h, mine, region(2, h), y_peer))
     for k in range(1, wide):
         start(copy(G + k, ids, all_ids.at[k], (me ^ k, core)))
         start(copy(G + wide + k, gains, all_gains.at[k], (me ^ k, core)))
@@ -279,40 +292,65 @@
                 for item in shared_copies(k):
                     item.start()
 
-    def stage(d):
-        landed(Z + d, region(PLANE * d))
-
-    def spread(d):
-        place = region(PLANE * d)
-        start(copy(X + d, place, region((PLANE * d) ^ 1), x_peer))
-        start(copy(Y + d, place, region((PLANE * d) ^ 2), y_peer))
-        start(copy(T + Z + d, place, place, twin))
-
-    def spread_if(where, d):
-        place = region(PLANE * d)
-        items = [
-            copy(X + d, place, region((PLANE * d) ^ 1), x_peer),
-            copy(Y + d, place, region((PLANE * d) ^ 2), y_peer),
-            copy(T + Z + d, place, place, twin),
+    def onward(d, h):
+        place = region(PLANE * d, h)
+        return [
+            copy(X + 2 * d + h, place, region((PLANE * d) ^ 1, h), x_peer),
+            copy(Y + 2 * d + h, place, region((PLANE * d) ^ 2, h), y_peer),
+            copy(T + Z + 2 * d + h, place, place, twin),
         ]
 
+    def stage(d, h):
+        landed(Z + 2 * d + h, region(PLANE * d, h))
+
+    def stage_if(where, d, h, then=()):
         @pl.when(where)
         def _():
-            for item in items:
+            stage(d, h)
+            for item in list(then) + onward(d, h):
                 item.start()
 
-    def beside(d):
-        k = 1 ^ (PLANE * d)
-        arrive(X + d, region(k))
-        start(copy(YD + d, region(k, 1), region(k ^ 2, 1), y_peer))
-        k = 2 ^ (PLANE * d)
-        arrive(Y + d, region(k))
-        start(copy(XD + d, region(k, 0), region(k ^ 1, 0), x_peer))
+    def spread(d, h):
+        for item in onward(d, h):
+            start(item)
+
+    def corner_rows(d, side):
+        if isinstance(d, int) and d == 1:
+            return {"begin": side * (half // 2), "size": half // 2}
+        return {"side": side}
+
+    def beside(d, axis, h):
+        k = (1 << axis) ^ (PLANE * d)
+        arrive((X, Y)[axis] + 2 * d + h, region(k, h))
+
+    def across_x(d):
+        k, rows_at = 2 ^ (PLANE * d), corner_rows(d, 0)
+        start(copy(XD + d, region(k, **rows_at), region(k ^ 1, **rows_at), x_peer))
+
+    def across_y(d):
+        k, rows_at = 1 ^ (PLANE * d), corner_rows(d, 1)
+        start(copy(YD + d, region(k, **rows_at), region(k ^ 2, **rows_at), y_peer))
+
+    def above(flip):
+        start(copy(B + flip, region(flip, 1), region(flip ^ PLANE, 1), near))
+
+    def above_if(where, flip):
+        @pl.when(where)
+        def _():
+            copy(B + flip, region(flip, 1), region(flip ^ PLANE, 1), near).start()
 
     def corner(d):
         k = 3 ^ (PLANE * d)
-        arrive(XD + d, region(k, 0))
-        arrive(YD + d, region(k, 1))
+        arrive(XD + d, region(k, **corner_rows(d, 0)))
+        arrive(YD + d, region(k, **corner_rows(d, 1)))
+
+    def corner_joined(d):
+        k = 3 ^ (PLANE * d)
+        for number, side in ((XD, 0), (YD, 1)):
+            joined(number + d, region(k, of=1 - core, **corner_rows(d, side)))
+
+    def half_joined(number, k, h):
+        joined(number + h, region(k, h, 1 - core))
 
     lane_r = lax.broadcasted_iota(jnp.int32, (count, count), 0)
     lane_c = lax.broadcasted_iota(jnp.int32, (count, count), 1)
@@ -324,6 +362,12 @@
 
     def block(k):
         return pl.ds(pl.multiple_of(k * count, count), count)
+
+    width = out.shape[1]
+
+    def halves():
+        for target, which in ((other, 1 - core), (acc, core)):
+            yield target, pl.ds(pl.multiple_of(which * width, width), width)
 
     def routed(ks):
         picks = []
@@ -341,30 +385,32 @@
             rows[place] = jnp.dot(
                 pick.astype(bf16), every[block(k)], preferred_element_type=f32
             ).astype(bf16)
-        gate_part = across(rows[...], w_gate[...])
-        up_part = across(rows[...], w_up[...])
-        hidden = (jax.nn.silu(gate_part) * up_part * slot_w[...]).astype(bf16)
+        live = pl.ds(0, len(ks) * slots)
+        gate_part = across(rows[live], w_gate[...])
+        up_part = across(rows[live], w_up[...])
+        hidden = (jax.nn.silu(gate_part) * up_part * slot_w[live]).astype(bf16)
         for b, k in enumerate(ks):
             back = jnp.dot(
                 picks[b].T.astype(bf16),
                 hidden[b * slots : (b + 1) * slots],
                 preferred_element_type=f32,
             )
-            both[block(k), LANES:] = back.astype(bf16)
-
-    width = out.shape[1]
+            both[block(k)] = back.astype(bf16)
+            for target, columns in halves():
+                target[block(k)] = jnp.dot(
+                    both[block(k)], w_down[:, columns], preferred_element_type=f32
+                ).astype(bf16)
 
     def partials(at):
         pre = jnp.dot(every[at], all_in[...], preferred_element_type=f32)
-        both[at, :LANES] = (jax.nn.silu(pre[:, :LANES]) * pre[:, LANES:]).astype(bf16)
-        for target, which in ((other, 1 - core), (acc, core)):
-            columns = pl.ds(pl.multiple_of(which * width, width), width)
-            part = jnp.dot(both[at], w_out[:, columns], preferred_element_type=f32)
-            target[at] = part.astype(bf16)
+        shared = (jax.nn.silu(pre[:, :LANES]) * pre[:, LANES:]).astype(bf16)
+        for target, columns in halves():
+            part = jnp.dot(shared, w_out[0:LANES, columns], preferred_element_type=f32)
+            target[at] = (target[at].astype(f32) + part).astype(bf16)
 
     second = jnp.where(inner, 3, 2)
     third = 5 - second
-    EARLY, MIDDLE = [], [12, 8, 13, 9, 14, 10, 15, 11]
+    EARLY = []
     send_shared(EARLY)
 
     @pl.when(my_piece < pieces)
@@ -383,79 +429,89 @@
         all_in[...] = jnp.zeros_like(all_in)
         w_out[0:LANES] = jnp.zeros((LANES, w_out.shape[1]), bf16)
 
-    stage(1)
-    start_inner(copy(Z + 2, region(PLANE), region(2 * PLANE), far, E + 1))
-    spread(1)
-
-    @pl.when(inner)
-    def _():
-        stage(3)
-        copy(Z + 2, region(3 * PLANE), region(2 * PLANE), near, E + 2).start()
-
-    spread_if(inner, 3)
-    beside(0)
+    outer = jnp.logical_not(inner)
+    for h in range(2):
+        stage(1, h)
+        start_inner(copy(Z + 4 + h, region(PLANE, h), region(2 * PLANE, h), far, E + 2 + h))
+        if h:
+            place = region(PLANE, h)
+            start(copy(T + Z + 2 + h, place, place, twin))
+        else:
+            spread(1, h)
+        back = copy(Z + 4 + h, region(3 * PLANE, h), region(2 * PLANE, h), near, E + 4 + h)
+        stage_if(inner, 3, h, [back])
+        beside(0, 0, h)
+        beside(0, 1, h)
+        if h:
+            across_y(0)
+            above_if(outer, 1)
+            above_if(outer, 2)
+        else:
+            across_x(0)
     for k in range(1, wide):
         landed(G + k, all_ids.at[k])
         landed(G + wide + k, all_gains.at[k])
     for item in loads:
         item.wait()
     own.wait()
-    joined(Z + 1, PLANE)
-    joined(X, 1)
-    joined(Y, 2)
+    for h in range(2):
+        half_joined(Z + 2, PLANE, h)
+        half_joined(X, 1, h)
+        half_joined(Y, 2, h)
+    for h in range(2):
+        stage_if(outer, 2, h)
+    beside(1, 0, 0)
+    across_y(1)
+    beside(1, 1, 0)
+    across_x(1)
+    for h in range(2):
+        more = copy(Z + 6 + h, region(2 * PLANE, h), region(3 * PLANE, h), near, E + 6 + h)
+        stage_if(inner, 2, h, [more])
+    above_if(inner, 1)
+    above_if(inner, 2)
+    corner(0)
+    above(3)
     routed([0, 1, 2, PLANE])
-
-    @pl.when(jnp.logical_not(inner))
-    def _():
-        stage(2)
-
-    spread_if(jnp.logical_not(inner), 2)
-    beside(1)
-    stage(third)
-    start_inner(copy(Z + 3, region(2 * PLANE), region(3 * PLANE), near, E + 3))
-    spread(third)
-    send_shared(MIDDLE)
-    corner(0)
-    joined(Z + second, PLANE * second)
-    joined(X + 1, PLANE ^ 1)
-    joined(Y + 1, PLANE ^ 2)
-    joined(XD, 3, 0)
-    joined(YD, 3, 1)
+    send_shared([12, 8, 13, 9, 14, 10, 15, 11])
+    for h in range(2):
+        stage_if(outer, 3, h)
+    for h in range(2):
+        beside(second, 0, h)
+        beside(second, 1, h)
+        if h:
+            across_y(second)
+        else:
+            across_x(second)
+    send_shared([5, 6, 7, 4, 3, 1, 2])
+    arrive(B + 1, region(1 ^ PLANE, 1))
+    arrive(B + 2, region(2 ^ PLANE, 1))
+    for h in range(2):
+        half_joined(Z + 2 * second, PLANE * second, h)
+    half_joined(X + 2, PLANE ^ 1, 0)
+    half_joined(Y + 2, PLANE ^ 2, 0)
+    joined(B + 1, region(1 ^ PLANE, 1, 1 - core))
+    joined(B + 2, region(2 ^ PLANE, 1, 1 - core))
+    corner_joined(0)
     routed([PLANE * second, PLANE ^ 1, PLANE ^ 2, 3])
-    beside(second)
-    beside(third)
-    send_shared([k for k in range(1, wide) if k not in EARLY + MIDDLE])
     corner(1)
-    joined(Z + third, PLANE * third)
-    joined(X + second, (PLANE * second) ^ 1)
-    joined(Y + second, (PLANE * second) ^ 2)
-    joined(XD + 1, 3 ^ PLANE, 0)
-    joined(YD + 1, 3 ^ PLANE, 1)
+    arrive(B + 3, region(3 ^ PLANE, 1))
+    for h in range(2):
+        beside(third, 0, h)
+        beside(third, 1, h)
+        if h:
+            across_y(third)
+        else:
+            across_x(third)
+    for h in range(2):
+        half_joined(Z + 2 * third, PLANE * third, h)
+        half_joined(X + 2 * second, (PLANE * second) ^ 1, h)
+        half_joined(Y + 2 * second, (PLANE * second) ^ 2, h)
+    corner_joined(1)
+    joined(B + 3, region(3 ^ PLANE, 1, 1 - core))
     routed([PLANE * third, (PLANE * second) ^ 1, (PLANE * second) ^ 2, 3 ^ PLANE])
-    corner(second)
-    corner(third)
-    joined(X + third, (PLANE * third) ^ 1)
-    joined(Y + third, (PLANE * third) ^ 2)
-    for d in (second, third):
-        joined(XD + d, 3 ^ (PLANE * d), 0)
-        joined(YD + d, 3 ^ (PLANE * d), 1)
-    routed(
-        [
-            (PLANE * third) ^ 1,
-            (PLANE * third) ^ 2,
-            3 ^ (PLANE * second),
-            3 ^ (PLANE * third),
-        ]
-    )
-    for k in range(1, wide):
-
-        @pl.when(my_piece < pieces)
-        def _():
-            for i, target in enumerate(places(me ^ k)):
-                landed(W + k + i * wide, target)
-
     RT, RXD, RYD = R, R + wide, R + wide + lines
-    RX, RY, RZ = RYD + lines, RYD + 2 * lines, RYD + 3 * lines
+    RX, RY, RZ = RYD + lines, RYD + 2 * lines, RC
+    RB = RZ + 10
     step = 16
 
     def rows_of(ref, k, begin=0, size=count):
@@ -483,53 +539,127 @@
         landed(RT + k, rows_of(twin_in, k))
         add(rows_of(acc, k), [rows_of(twin_in, k)])
 
-    tall = count // 2
+    def cut(d):
+        low = (0,) + tuple(count // part for part in (4, 4, 4))
+        low = low[d]
+        return low, (count - low) // 2
+
+    def by_line(flip, d):
+        low, number = cut(d)[0], 3 * (flip - 1) + d - 1
+        if not low:
+            return
+        start(
+            copy(
+                RB + number,
+                rows_of(acc, flip ^ (PLANE * d), 0, low),
+                plane_in.at[number, pl.ds(0, low)],
+                (me ^ (PLANE * d), core),
+            )
+        )
+
+    def from_line(flip):
+        for d in range(1, lines):
+            low, number = cut(d)[0], 3 * (flip - 1) + d - 1
+            if low:
+                place = plane_in.at[number, pl.ds(0, low)]
+                landed(RB + number, place)
+                add(rows_of(acc, flip, 0, low), [place])
 
     def diagonal(d):
         k = 3 ^ (PLANE * d)
+        low, tall = cut(d)
         fold(k)
-        start(copy(RXD + d, rows_of(acc, k, 0, tall), diag_in.at[0, d], x_peer))
-        start(copy(RYD + d, rows_of(acc, k, tall, tall), diag_in.at[1, d], y_peer))
+        if d:
+            by_line(3, d)
+        else:
+            from_line(3)
+        place = pl.ds(0, tall)
+        start(copy(RXD + d, rows_of(acc, k, low, tall), diag_in.at[0, d, place], x_peer))
+        start(copy(RYD + d, rows_of(acc, k, low + tall, tall), diag_in.at[1, d, place], y_peer))
 
     def sides(d):
+        low, tall = cut(d)
+        place, rest = pl.ds(0, tall), pl.ds(low, 2 * tall)
+        for flip in (2, 1):
+            fold(flip ^ (PLANE * d))
+            if d:
+                by_line(flip, d)
+            else:
+                from_line(flip)
         k = 2 ^ (PLANE * d)
-        fold(k)
-        landed(RXD + d, diag_in.at[0, d])
-        add(rows_of(acc, k, 0, tall), [diag_in.at[0, d]])
-        start(copy(RY + d, rows_of(acc, k), side_in.at[1, d], y_peer))
+        landed(RXD + d, diag_in.at[0, d, place])
+        add(rows_of(acc, k, low, tall), [diag_in.at[0, d, place]])
+        start(copy(RY + d, rows_of(acc, k, low, 2 * tall), side_in.at[1, d, rest], y_peer))
         k = 1 ^ (PLANE * d)
-        fold(k)
-        landed(RYD + d, diag_in.at[1, d])
-        add(rows_of(acc, k, tall, tall), [diag_in.at[1, d]])
-        start(copy(RX + d, rows_of(acc, k), side_in.at[0, d], x_peer))
+        landed(RYD + d, diag_in.at[1, d, place])
+        add(rows_of(acc, k, low + tall, tall), [diag_in.at[1, d, place]])
+        start(copy(RX + d, rows_of(acc, k, low, 2 * tall), side_in.at[0, d, rest], x_peer))
 
     near_in, far_in, far_out = line_in.at[0], line_in.at[1], line_in.at[2]
 
     def upright(d):
         k = PLANE * d
+        low, tall = cut(d)
+        rest = pl.ds(low, 2 * tall)
         fold(k)
-        landed(RX + d, side_in.at[0, d])
-        landed(RY + d, side_in.at[1, d])
-        add(rows_of(acc, k), [side_in.at[0, d], side_in.at[1, d]])
+        landed(RX + d, side_in.at[0, d, rest])
+        landed(RY + d, side_in.at[1, d, rest])
+        add(rows_of(acc, k, low, 2 * tall), [side_in.at[0, d, rest], side_in.at[1, d, rest]])
+
+    def legs(number, k, place, to):
+        size = count // 2
+        return [
+            copy(
+                RZ + 2 * number + h,
+                rows_of(acc, k, h * size, size),
+                place.at[pl.ds(h * size, size)],
+                to,
+            )
+            for h in range(2)
+        ]
 
     def outward(number, k, place):
-        item = copy(RZ + number, rows_of(acc, k), place, near)
-        outer_started.append(item)
-
-        @pl.when(jnp.logical_not(inner))
-        def _():
-            item.start()
-
-    def inward(number, place, k, item):
-        inner_started.append(item)
+        for item in legs(number, k, place, near):
+            outer_started.append(item)
+
+            @pl.when(outer)
+            def _():
+                item.start()
+
+    def inward(number, place, k, items):
+        inner_started.extend(items)
+        size = count // 2
 
         @pl.when(inner)
         def _():
-            landed(RZ + number, place)
-            add(rows_of(acc, k), [place])
-            item.start()
+            for h, item in enumerate(items):
+                part = place.at[pl.ds(h * size, size)]
+                landed(RZ + 2 * number + h, part)
+                add(rows_of(acc, k, h * size, size), [part])
+                item.start()
+
+    def leg_landed(number, place):
+        size = count // 2
+        for h in range(2):
+            landed(RZ + 2 * number + h, place.at[pl.ds(h * size, size)])
 
     one, two, three = PLANE, 2 * PLANE, 3 * PLANE
+    for h in range(2):
+        half_joined(X + 2 * third, (PLANE * third) ^ 1, h)
+        half_joined(Y + 2 * third, (PLANE * third) ^ 2, h)
+    routed([(PLANE * third) ^ 1, (PLANE * third) ^ 2])
+    corner(second)
+    corner(third)
+    corner_joined(second)
+    corner_joined(third)
+    routed([3 ^ (PLANE * second), 3 ^ (PLANE * third)])
+    for k in range(1, wide):
+
+        @pl.when(my_piece < pieces)
+        def _():
+            for i, target in enumerate(places(me ^ k)):
+                landed(W + k + i * wide, target)
+
     compute(3, [3])
     compute(2, [3])
     diagonal(3)
@@ -548,25 +678,25 @@
     diagonal(0)
     compute(1, [1, 2])
     sides(1)
-    compute(1, [0])
     upright(2)
     outward(1, two, far_in)
-    inward(0, near_in, two, copy(RZ + 2, rows_of(acc, two), far_out, far))
+    compute(1, [0])
+    inward(0, near_in, two, legs(2, two, far_out, far))
     compute(0, [1, 2])
     sides(0)
-    compute(0, [0])
-    inward(1, far_in, three, copy(RZ + 3, rows_of(acc, three), line_in.at[3], far))
     upright(1)
     outward(4, one, line_in.at[4])
-    inward(2, far_out, one, copy(RZ + 4, rows_of(acc, one), line_in.at[4], near))
+    compute(0, [0])
+    inward(1, far_in, three, legs(3, three, line_in.at[3], far))
+    inward(2, far_out, one, legs(4, one, line_in.at[4], near))
     upright(0)
 
     @pl.when(inner)
     def _():
-        landed(RZ + 3, line_in.at[3])
+        leg_landed(3, line_in.at[3])
         add(rows_of(acc, 0), [line_in.at[3]])
 
-    landed(RZ + 4, line_in.at[4])
+    leg_landed(4, line_in.at[4])
 
     def last(i, carry):
         at = pl.ds(pl.multiple_of(i * step, step), step)
@@ -585,14 +715,19 @@
     for item in started:
         item.wait_send()
 
-    place = region(PLANE * second)
-    copy(X + second, place, region((PLANE * second) ^ 1), x_peer).wait_send()
-    copy(Y + second, place, region((PLANE * second) ^ 2), y_peer).wait_send()
-    copy(T + Z + second, place, place, twin).wait_send()
+    for h in range(2):
+        for item in onward(second, h) + onward(third, h):
+            item.wait_send()
+    for flip in (1, 2):
+        copy(B + flip, region(flip, 1), region(flip ^ PLANE, 1), near).wait_send()
 
     @pl.when(inner)
     def _():
-        copy(Z + 2, region(3 * PLANE), region(2 * PLANE), near, E + 2).wait_send()
+        for h in range(2):
+            back = copy(Z + 4 + h, region(3 * PLANE, h), region(2 * PLANE, h), near, E + 4 + h)
+            back.wait_send()
+            more = copy(Z + 6 + h, region(2 * PLANE, h), region(3 * PLANE, h), near, E + 6 + h)
+            more.wait_send()
         for item in inner_started:
             item.wait_send()
 
@@ -607,7 +742,7 @@
     part = width // narrow
     lines = wide // PLANE
     total = wide * count
-    sems = 10 * lines + 6 * wide + 4 * lines + 5 + 4
+    sems = 22 * lines + 6 * wide + 10 + 9 + 8
     bf16, f32 = jnp.bfloat16, jnp.float32
     return pl.pallas_call(
         functools.partial(fused_kernel, wide, slots),
@@ -624,13 +759,14 @@
             pltpu.VMEM((LANES + w_down.shape[0], w_down.shape[1]), bf16),
             pltpu.VMEM((lines * slots, width), bf16),
             pltpu.VMEM((lines * slots, 1), f32),
-            pltpu.VMEM((total, LANES + w_gate.shape[0]), bf16),
+            pltpu.VMEM((total, w_gate.shape[0]), bf16),
             pltpu.VMEM((total, part), bf16),
             pltpu.VMEM((total, part), bf16),
             pltpu.VMEM((total, part), bf16),
             pltpu.VMEM((2, lines, count // 2, part), bf16),
             pltpu.VMEM((2, lines, count, part), bf16),
             pltpu.VMEM((5, count, part), bf16),
+            pltpu.VMEM((3 * (lines - 1), count // 2, part), bf16),
             pltpu.SemaphoreType.DMA((sems,)),
             pltpu.SemaphoreType.DMA((sems,)),
             pltpu.SemaphoreType.DMA((9,)),

time: 110 us -> 103 us (0.936)
  Pallas kernels: 108 us -> 102 us
    pallas_call x1, Pallas kernels: 108 us -> 102 us  [fused(): pl.pallas_call(functools.partial(fused_kernel, wide, slots), out_shape=ja...]
where the time goes in v2:
time: 103 us
  Pallas kernels  102 us (99%)
  local copies, waits for them, and re-layouts  1.67 us (2%)
    pallas_call x1, Pallas kernels, fused(): pl.pallas_call(functools.partial(fused_kernel, wide, slots), out_shape=ja...  102 us

profile of v2, /device:TPU:0, one launch (start us, length us, event | category | flops | bytes accessed | tf_op | source)
XLA Modules:
  0.0 103.2 jit_solution(12217747865664202300)
XLA Ops:
  0.0 101.5 %shard_map.91 = bf16[128,1024]{1,0:T(8,128)(2,1)} custom-call(bf16[128,2048]{1,0:T(8,128)(2,1)} %tok.1, s32[6,128]{1,0:T(8,128)} %bitcast.12, f32[6,128]{1,0:T(8,128)} %bitcast.13, bf16[128,1408]{1,0:T(8,128)(2,1)} %gate.1, bf16[128,1408]{1,0:T(8,128)(2,1)} %up.1, bf16[1408,128]{1,0:T(8,128)(2,1)} %down.1, bf16[704,2048]{1,0:T(8,128)(2,1)} %bitcast.9, ...), custom_call_target="tpu_custom_call" | custom-call | tf_op jit(solution)/shard_map/pallas_call | solution.py:747
  101.5 1.7 %copy.11 = bf16[128,1024]{1,0:T(8,128)(2,1)} copy(bf16[128,1024]{1,0:T(8,128)(2,1)} %shard_map.91) | data formatting | bytes 524288

commit v3 on v2

--- a/solution.py
+++ b/solution.py
@@ -680,8 +680,8 @@
     sides(1)
     upright(2)
     outward(1, two, far_in)
+    inward(0, near_in, two, legs(2, two, far_out, far))
     compute(1, [0])
-    inward(0, near_in, two, legs(2, two, far_out, far))
     compute(0, [1, 2])
     sides(0)
     upright(1)

time: 103 us -> 103 us (level)
  no operation moved by 1% of the time
where the time goes in v3:
time: 103 us
  Pallas kernels  102 us (99%)
  local copies, waits for them, and re-layouts  1.67 us (2%)
    pallas_call x1, Pallas kernels, fused(): pl.pallas_call(functools.partial(fused_kernel, wide, slots), out_shape=ja...  102 us

profile of v3, /device:TPU:0, one launch (start us, length us, event | category | flops | bytes accessed | tf_op | source)
XLA Modules:
  0.0 103.3 jit_solution(3142887795169276878)
XLA Ops:
  0.0 101.6 %shard_map.91 = bf16[128,1024]{1,0:T(8,128)(2,1)} custom-call(bf16[128,2048]{1,0:T(8,128)(2,1)} %tok.1, s32[6,128]{1,0:T(8,128)} %bitcast.12, f32[6,128]{1,0:T(8,128)} %bitcast.13, bf16[128,1408]{1,0:T(8,128)(2,1)} %gate.1, bf16[128,1408]{1,0:T(8,128)(2,1)} %up.1, bf16[1408,128]{1,0:T(8,128)(2,1)} %down.1, bf16[704,2048]{1,0:T(8,128)(2,1)} %bitcast.9, ...), custom_call_target="tpu_custom_call" | custom-call | tf_op jit(solution)/shard_map/pallas_call | solution.py:747
  101.6 1.7 %copy.11 = bf16[128,1024]{1,0:T(8,128)(2,1)} copy(bf16[128,1024]{1,0:T(8,128)(2,1)} %shard_map.91) | data formatting | bytes 524288
